TPU v7x, 32 devices: a whole 2x2x4 slice. The times are simulated.
32 devices in a mesh: rows: 8 (over z, x), cols: 4 (over y, core).
Axes of the slice: x: 2, y: 2, z: 4, core: 2. Of those that a mesh axis runs over, the one named last changes fastest.
Arguments:
- coupling: float32 [2, 16384, 16384], P(None, 'rows', 'cols'), may hold values from -2 to 40, as said below
- initial: float32 [2, 48, 16384], P(None, None, 'rows'), may hold values from -8 to 8
Outputs:
- basis: float32 [2, 48, 16384], P(None, None, ('rows', 'cols'))
- ritz: float32 [4, 2, 48, 48], replicated
Inputs may be any that keep to these rules, and one draw needn't show every extreme that they name: `coupling`: H is Hermitian (the first plane symmetric, the second antisymmetric) and positive definite.
All inputs are finite; a program needn't handle non-finite values.
Results may differ from a plain program's by a relative error of at most 0.0003.
Values sent between devices are 32-bit elements; how exact they have to be, the bound alone decides.
No kernel may reach another device: no remote copies, remote signals or barrier semaphores. Data moves between devices by JAX's collectives and lax.ppermute only.
A program may use at most 128 MiB of HBM per device.

v0:
```python
import jax
import jax.numpy as jnp
from jax import lax
from jax.sharding import PartitionSpec as P

N = 16384
ITERS = 4
HIGH = lax.Precision.HIGHEST


def pair_products(left, right):
    real_part = jnp.dot(left[0], right[0].T, precision=HIGH) + jnp.dot(
        left[1], right[1].T, precision=HIGH
    )
    imag_part = jnp.dot(left[0], right[1].T, precision=HIGH) - jnp.dot(
        left[1], right[0].T, precision=HIGH
    )
    return jnp.stack([real_part, imag_part])


def orthonormal(gram_matrix, images):
    gram_re = gram_matrix[0]
    gram_im = gram_matrix[1]
    vectors = gram_re.shape[0]
    width = images.shape[2]
    upper_pair = jnp.stack([gram_re, -gram_im], axis=-1)
    lower_pair = jnp.stack([gram_im, gram_re], axis=-1)
    embedded = jnp.stack([upper_pair, lower_pair], axis=1).reshape(2 * vectors, 2 * vectors)
    factor = jnp.linalg.cholesky(embedded)
    woven = jnp.transpose(images, (1, 0, 2)).reshape(2 * vectors, width)
    solved = lax.linalg.triangular_solve(factor, woven, left_side=True, lower=True)
    return jnp.transpose(solved.reshape(vectors, 2, width), (1, 0, 2))


def tile_product(coupling, local_block):
    vectors = local_block.shape[1]
    stacked = local_block.reshape(2 * vectors, local_block.shape[2])
    contract = (((1,), (1,)), ((), ()))
    with_real = lax.dot_general(
        stacked, coupling[0], contract, precision=HIGH, preferred_element_type=jnp.float32
    )
    with_imag = lax.dot_general(
        stacked, coupling[1], contract, precision=HIGH, preferred_element_type=jnp.float32
    )
    return jnp.stack(
        [with_real[:vectors] - with_imag[vectors:], with_real[vectors:] + with_imag[:vectors]]
    )


def body(coupling, initial):
    row_width = initial.shape[2]
    per_column = lax.axis_size("rows") // lax.axis_size("cols")
    column = lax.axis_index("cols")
    block_span = row_width * per_column
    piece_width = row_width // lax.axis_size("cols")
    order_value = float(N)
    ritz_list = []
    current = lax.dynamic_slice_in_dim(initial, column * piece_width, piece_width, 2)
    for iteration in range(ITERS):
        gathered = lax.all_gather(current, ("rows", "cols"), axis=2, tiled=True)
        local_block = lax.dynamic_slice_in_dim(gathered, column * block_span, block_span, 2)
        partial_value = tile_product(coupling, local_block)
        images = lax.psum_scatter(partial_value, "cols", scatter_dimension=2, tiled=True)
        gram_matrix, projection = lax.psum(
            (pair_products(images, images), pair_products(current, images)), ("rows", "cols")
        )
        ritz_list.append(projection / order_value)
        current = orthonormal(gram_matrix / order_value, images)
    return (current, jnp.stack(ritz_list))


def solution(mesh):
    placed = (P(None, "rows", "cols"), P(None, None, "rows"))
    return jax.shard_map(
        body,
        mesh=mesh,
        in_specs=placed,
        out_specs=(P(None, None, ("rows", "cols")), P()),
        check_vma=False,
    )
```

profile of v0, /device:TPU:0, one launch (start us, length us, event | category | flops | bytes accessed | tf_op | source)
XLA Modules:
  0.0 1063.4 jit_solution(4548301341809468267)
XLA Ops:
  7.2 1.1 copy-done
  9.1 74.6 %all-gather.5.cloned.1.call-done = f32[2,48,16384]{2,1,0:T(8,128)} async-done(((f32[2,48,512]{2,1,0:T(8,128)}), f32[2,48,16384]{2,1,0:T(8,128)}) %all-gather.5.cloned.1.call-update) | async-done | bytes 6291472 | tf_op jit(solution)/shard_map/all_gather | solution.py:60
  83.7 1.5 constant_dynamic-slice_fusion.3
  85.2 36.0 %fusion.6 = f32[96,2048]{1,0:T(8,128)S(1)} fusion(f32[96,4096]{1,0:T(8,128)S(1)} %bitcast.280, f32[2,2048,4096]{2,1,0:T(8,128)} %param.5), kind=kOutput, calls=%fused_computation.6 | convolution fusion | flops 9663676416 | bytes 35913728 | tf_op jit(solution)/shard_map/dot_general | solution.py:42
  121.2 36.8 %fusion.14 = f32[96,2048]{1,0:T(8,128)} fusion(f32[96,4096]{1,0:T(8,128)S(1)} %bitcast.281, f32[2,2048,4096]{2,1,0:T(8,128)} %param.5), kind=kOutput, calls=%fused_computation.14 | convolution fusion | flops 9663676416 | bytes 35913728 | tf_op jit(solution)/shard_map/dot_general | solution.py:39
  158.0 1.2 fusion.47
  160.3 22.1 %reduce-scatter.5.cloned.1.call-done = f32[2,48,512]{2,1,0:T(8,128)} async-done(((f32[2,48,2048]{2,1,0:T(8,128)}), f32[2,48,512]{2,1,0:T(8,128)}) %reduce-scatter.5.cloned.1.call-update) | async-done | bytes 196624 | tf_op jit(solution)/shard_map/reduce_scatter | solution.py:63
  182.4 1.2 fusion.56
  183.5 1.2 fusion.57
  184.7 1.2 fusion.38
  185.9 1.2 fusion.39
  187.1 40.3 %psum.56 = f32[2,48,48]{2,1,0:T(8,128)S(1)} all-reduce(f32[2,48,48]{2,1,0:T(8,128)S(1)} %pad_maximum_fusion.9), channel_id=1, replica_groups=mesh['rows'=8,'cols'=4] {'rows','cols'}, use_global_device_ids=true, to_apply=%region_1.0 | all-reduce | flops 4608 | bytes 36864 | tf_op jit(solution)/shard_map/psum | solution.py:64
  227.5 1.1 copy.15
  230.7 8.8 cholesky.74
  240.8 7.4 custom-call.8
  249.4 70.3 %all-gather.7.cloned.1.call-done = f32[2,48,16384]{2,1,0:T(8,128)} async-done(((f32[2,48,512]{2,1,0:T(8,128)}), f32[2,48,16384]{2,1,0:T(8,128)}) %all-gather.7.cloned.1.call-update) | async-done | bytes 6291472 | tf_op jit(solution)/shard_map/all_gather | solution.py:60
  319.8 1.5 constant_dynamic-slice_fusion.2
  321.3 36.1 %fusion.4 = f32[96,2048]{1,0:T(8,128)S(1)} fusion(f32[96,4096]{1,0:T(8,128)S(1)} %bitcast.282, f32[2,2048,4096]{2,1,0:T(8,128)} %param.5), kind=kOutput, calls=%fused_computation.4 | convolution fusion | flops 9663676416 | bytes 35913728 | tf_op jit(solution)/shard_map/dot_general | solution.py:42
  357.4 36.7 %fusion.12 = f32[96,2048]{1,0:T(8,128)} fusion(f32[96,4096]{1,0:T(8,128)S(1)} %bitcast.283, f32[2,2048,4096]{2,1,0:T(8,128)} %param.5), kind=kOutput, calls=%fused_computation.12 | convolution fusion | flops 9663676416 | bytes 35913728 | tf_op jit(solution)/shard_map/dot_general | solution.py:39
  394.1 1.2 fusion.45
  396.4 22.1 %reduce-scatter.7.cloned.1.call-done = f32[2,48,512]{2,1,0:T(8,128)} async-done(((f32[2,48,2048]{2,1,0:T(8,128)}), f32[2,48,512]{2,1,0:T(8,128)}) %reduce-scatter.7.cloned.1.call-update) | async-done | bytes 196624 | tf_op jit(solution)/shard_map/reduce_scatter | solution.py:63
  418.5 1.2 fusion.58
  419.6 1.2 fusion.59
  420.8 1.2 fusion.36
  422.0 1.2 fusion.37
  423.2 39.9 %psum.57 = f32[2,48,48]{2,1,0:T(8,128)S(1)} all-reduce(f32[2,48,48]{2,1,0:T(8,128)S(1)} %pad_maximum_fusion.10), channel_id=1, replica_groups=mesh['rows'=8,'cols'=4] {'rows','cols'}, use_global_device_ids=true, to_apply=%region_5.8 | all-reduce | flops 4608 | bytes 36864 | tf_op jit(solution)/shard_map/psum | solution.py:64
  463.2 1.1 copy.19
  466.4 8.8 cholesky.85
  476.6 7.4 custom-call.9
  485.2 70.3 %all-gather.9.cloned.1.call-done = f32[2,48,16384]{2,1,0:T(8,128)} async-done(((f32[2,48,512]{2,1,0:T(8,128)}), f32[2,48,16384]{2,1,0:T(8,128)}) %all-gather.9.cloned.1.call-update) | async-done | bytes 6291472 | tf_op jit(solution)/shard_map/all_gather | solution.py:60
  555.5 1.5 constant_dynamic-slice_fusion.1
  557.0 36.3 %fusion.2 = f32[96,2048]{1,0:T(8,128)S(1)} fusion(f32[96,4096]{1,0:T(8,128)S(1)} %bitcast.284, f32[2,2048,4096]{2,1,0:T(8,128)} %param.5), kind=kOutput, calls=%fused_computation.2 | convolution fusion | flops 9663676416 | bytes 35913728 | tf_op jit(solution)/shard_map/dot_general | solution.py:42
  593.3 37.0 %fusion.10 = f32[96,2048]{1,0:T(8,128)} fusion(f32[96,4096]{1,0:T(8,128)S(1)} %bitcast.285, f32[2,2048,4096]{2,1,0:T(8,128)} %param.5), kind=kOutput, calls=%fused_computation.10 | convolution fusion | flops 9663676416 | bytes 35913728 | tf_op jit(solution)/shard_map/dot_general | solution.py:39
  630.3 1.2 fusion.43
  632.6 22.1 %reduce-scatter.9.cloned.1.call-done = f32[2,48,512]{2,1,0:T(8,128)} async-done(((f32[2,48,2048]{2,1,0:T(8,128)}), f32[2,48,512]{2,1,0:T(8,128)}) %reduce-scatter.9.cloned.1.call-update) | async-done | bytes 196624 | tf_op jit(solution)/shard_map/reduce_scatter | solution.py:63
  654.7 1.2 fusion.60
  655.8 1.2 fusion.61
  657.1 1.2 fusion.34
  658.2 1.2 fusion.35
  659.4 39.9 %psum.58 = f32[2,48,48]{2,1,0:T(8,128)S(1)} all-reduce(f32[2,48,48]{2,1,0:T(8,128)S(1)} %pad_maximum_fusion.11), channel_id=1, replica_groups=mesh['rows'=8,'cols'=4] {'rows','cols'}, use_global_device_ids=true, to_apply=%region_7.10 | all-reduce | flops 4608 | bytes 36864 | tf_op jit(solution)/shard_map/psum | solution.py:64
  699.4 1.1 copy.23
  701.3 1.7 copy.21
  702.9 1.5 reshape.112
  706.1 8.8 cholesky.96
  716.2 7.4 custom-call.10
  726.4 68.7 %all-gather.11.cloned.1.call-done = f32[2,48,16384]{2,1,0:T(8,128)} async-done(((f32[2,48,512]{2,1,0:T(8,128)}), f32[2,48,16384]{2,1,0:T(8,128)}) %all-gather.11.cloned.1.call-update) | async-done | bytes 6291472 | tf_op jit(solution)/shard_map/all_gather | solution.py:60
  795.1 1.5 constant_dynamic-slice_fusion
  796.7 36.7 %fusion = f32[96,2048]{1,0:T(8,128)} fusion(f32[96,4096]{1,0:T(8,128)S(1)} %bitcast.278, f32[2,2048,4096]{2,1,0:T(8,128)} %param.5), kind=kOutput, calls=%fused_computation | convolution fusion | flops 9663676416 | bytes 35913728 | tf_op jit(solution)/shard_map/dot_general | solution.py:42
  833.4 36.8 %fusion.8 = f32[96,2048]{1,0:T(8,128)} fusion(f32[96,4096]{1,0:T(8,128)S(1)} %bitcast.279, f32[2,2048,4096]{2,1,0:T(8,128)} %param.5), kind=kOutput, calls=%fused_computation.8 | convolution fusion | flops 9663676416 | bytes 35913728 | tf_op jit(solution)/shard_map/dot_general | solution.py:39
  870.2 1.5 fusion.41
  876.2 18.7 %reduce-scatter.11.cloned.1.call-done = f32[2,48,512]{2,1,0:T(8,128)} async-done(((f32[2,48,2048]{2,1,0:T(8,128)}), f32[2,48,512]{2,1,0:T(8,128)}) %reduce-scatter.11.cloned.1.call-update) | async-done | bytes 196624 | tf_op jit(solution)/shard_map/reduce_scatter | solution.py:63
  894.9 1.1 fusion.52
  896.0 1.1 fusion.53
  897.1 1.1 fusion.24
  898.2 1.1 fusion.25
  900.0 1.2 fusion.62
  901.2 1.2 fusion.63
  902.4 1.2 fusion.32
  903.6 1.2 fusion.33
  905.4 1.1 copy.27
  906.6 126.8 %all-reduce.3.cloned.1.call-done = (f32[2,48,48]{2,1,0:T(8,128)}, f32[2,48,48]{2,1,0:T(8,128)}, f32[2,48,48]{2,1,0:T(8,128)}, f32[2,48,48]{2,1,0:T(8,128)}, f32[2,48,48]{2,1,0:T(8,128)}) async-done(((f32[2,48,48]{2,1,0:T(8,128)}, f32[2,48,48]{2,1,0:T(8,128)}, f32[2,48,48]{2,1,0:T(8,128)}, f32[2,48,48]{2,1,0:T(8,128)}, f32[2,48,48]{2,1,0:T(8,128)}), (f32[2,48,48]{2,1,0:T(8,128)}, f32[2,48,48]{2,1,0:T(8,128)}, ...) | async-done | bytes 92176 | tf_op jit(solution)/shard_map/psum | solution.py:64
  1035.2 1.0 reshape.116
  1036.3 8.8 cholesky.107
  1046.4 7.4 custom-call.11
  (124 shorter events, 31.5 us)
Async XLA Ops:
  7.2 1.1 copy-start
  7.2 76.5 %all-gather.5.cloned.1.call-start = ((), (), s32[]{:S(2)}) async-start(), calls=%async_computation.4 | async-start | bytes 6488064 | tf_op jit(solution)/shard_map/all_gather | solution.py:60
  9.0 173.3 %reduce-scatter.5.cloned.1.call-start = ((), (), s32[]{:S(2)}) async-start(), calls=%async_computation.5 | async-start | bytes 983040 | tf_op jit(solution)/shard_map/reduce_scatter | solution.py:63
  160.2 159.5 %all-gather.7.cloned.1.call-start = ((), (), s32[]{:S(2)}) async-start(), calls=%async_computation.6 | async-start | bytes 6488064 | tf_op jit(solution)/shard_map/all_gather | solution.py:60
  249.4 169.1 %reduce-scatter.7.cloned.1.call-start = ((), (), s32[]{:S(2)}) async-start(), calls=%async_computation.7 | async-start | bytes 983040 | tf_op jit(solution)/shard_map/reduce_scatter | solution.py:63
  396.3 159.2 %all-gather.9.cloned.1.call-start = ((), (), s32[]{:S(2)}) async-start(), calls=%async_computation.8 | async-start | bytes 6488064 | tf_op jit(solution)/shard_map/all_gather | solution.py:60
  485.2 169.5 %reduce-scatter.9.cloned.1.call-start = ((), (), s32[]{:S(2)}) async-start(), calls=%async_computation.9 | async-start | bytes 983040 | tf_op jit(solution)/shard_map/reduce_scatter | solution.py:63
  631.5 93.3 %copy-start.1 = (f32[2,48,512]{2,1,0:T(8,128)S(1)}, f32[2,48,512]{2,1,0:T(8,128)}, u32[]{:S(2)}) copy-start(f32[2,48,512]{2,1,0:T(8,128)} %reduce-scatter.5.cloned.1.call-done) | copy-start | bytes 589828
  632.5 162.6 %all-gather.11.cloned.1.call-start = ((), (), s32[]{:S(2)}) async-start(), calls=%async_computation.10 | async-start | bytes 6488064 | tf_op jit(solution)/shard_map/all_gather | solution.py:60
  724.8 170.0 %reduce-scatter.11.cloned.1.call-start = ((), (), s32[]{:S(2)}) async-start(), calls=%async_computation.11 | async-start | bytes 983040 | tf_op jit(solution)/shard_map/reduce_scatter | solution.py:63
  833.4 39.7 %copy-start.2 = (f32[2,48,512]{2,1,0:T(8,128)S(1)}, f32[2,48,512]{2,1,0:T(8,128)}, u32[]{:S(2)}) copy-start(f32[2,48,512]{2,1,0:T(8,128)} %reduce-scatter.7.cloned.1.call-done) | copy-start | bytes 589828
  833.4 39.7 %copy-start.4 = (f32[48,2,512]{2,0,1:T(8,128)S(1)}, f32[48,2,512]{2,0,1:T(8,128)}, u32[]{:S(2)}) copy-start(f32[48,2,512]{2,0,1:T(8,128)} %copy.36) | copy-start | bytes 589828
  833.4 41.3 %copy-start.3 = (f32[2,48,512]{2,1,0:T(8,128)S(1)}, f32[2,48,512]{2,1,0:T(8,128)}, u32[]{:S(2)}) copy-start(f32[2,48,512]{2,1,0:T(8,128)} %reduce-scatter.9.cloned.1.call-done) | copy-start | bytes 589828
  833.4 41.3 %copy-start.5 = (f32[48,2,512]{2,0,1:T(8,128)S(1)}, f32[48,2,512]{2,0,1:T(8,128)}, u32[]{:S(2)}) copy-start(f32[48,2,512]{2,0,1:T(8,128)} %copy.35) | copy-start | bytes 589828
  870.2 24.6 %copy-start.6 = (f32[48,2,512]{2,0,1:T(8,128)S(1)}, f32[48,2,512]{2,0,1:T(8,128)}, u32[]{:S(2)}) copy-start(f32[48,2,512]{2,0,1:T(8,128)} %copy.34) | copy-start | bytes 589828
  872.7 160.8 %all-reduce.3.cloned.1.call-start = ((), (), s32[]{:S(2)}) async-start(), calls=%async_computation.12 | async-start | bytes 491520 | tf_op jit(solution)/shard_map/psum | solution.py:64
  1033.5 22.3 %copy-start.7 = (f32[2,48,48]{2,1,0:T(8,128)S(1)}, f32[2,48,48]{2,1,0:T(8,128)}, u32[]{:S(2)}) copy-start(f32[2,48,48]{2,1,0:T(8,128)} %get-tuple-element.7) | copy-start | bytes 55300
  1033.5 22.4 %copy-start.8 = (f32[2,48,48]{2,1,0:T(8,128)S(1)}, f32[2,48,48]{2,1,0:T(8,128)}, u32[]{:S(2)}) copy-start(f32[2,48,48]{2,1,0:T(8,128)} %get-tuple-element.8) | copy-start | bytes 55300
Sparse Core Ops, SparseCore 0:
  11.5 72.1 all-gather.4
  160.3 21.9 reduce-scatter.4
  249.5 70.1 all-gather.6
  396.4 21.9 reduce-scatter.6
  485.3 70.2 all-gather.8
  632.6 21.9 reduce-scatter.8
  724.9 70.1 all-gather.10
  872.8 21.9 reduce-scatter.10
  905.5 127.9 all-reduce.2
where the time goes:
time: 1070 us; the launch traced here: 1060 us
  waiting for transfers between devices  496 us (46%)
  matrix products  320 us (30%)
  blocking collectives  120 us (11%)
  other arithmetic  85.8 us (8%)
  local copies, waits for them, and re-layouts  25.8 us (2%)
  between operations  14.9 us (1%)
    all_gather x4, waiting for transfers between devices, body(): gathered = lax.all_gather(current, ('rows', 'cols'), axis=2, tiled=True)  284 us
    dot_general x4, matrix products, tile_product(): lax.dot_general(stacked, coupling[0], contract, precision=HIGH, preferred...  147 us
    dot_general x4, matrix products, tile_product(): lax.dot_general(stacked, coupling[1], contract, precision=HIGH, preferred...  145 us
    psum x1, waiting for transfers between devices, body(): lax.psum((pair_products(images, images), pair_products(current, images)),...  127 us
    psum x3, blocking collectives, body(): lax.psum((pair_products(images, images), pair_products(current, images)),...  120 us
    reduce_scatter x4, waiting for transfers between devices, body(): lax.psum_scatter(partial_value, 'cols', scatter_dimension=2, tiled=True)  85 us
    another operation x12, other arithmetic, orthonormal(): factor = jnp.linalg.cholesky(embedded)  37.9 us
    another operation x8, other arithmetic, orthonormal(): lax.linalg.triangular_solve(factor, woven, left_side=True, lower=True)  32 us
  transfers between devices with their start and end apart: 9, of which 9 were waited for; matrix products, arithmetic and copies ran while one was open for 1% of the time, Pallas kernels for 0%

commit v1 on v0

--- a/solution.py
+++ b/solution.py
@@ -57,7 +57,12 @@
     ritz_list = []
     current = lax.dynamic_slice_in_dim(initial, column * piece_width, piece_width, 2)
     for iteration in range(ITERS):
-        gathered = lax.all_gather(current, ("rows", "cols"), axis=2, tiled=True)
+        gathered = jnp.concatenate(
+            lax.all_to_all(
+                jnp.stack([current] * lax.axis_size(("rows", "cols"))), ("rows", "cols"), 0, 0
+            ),
+            axis=2,
+        )
         local_block = lax.dynamic_slice_in_dim(gathered, column * block_span, block_span, 2)
         partial_value = tile_product(coupling, local_block)
         images = lax.psum_scatter(partial_value, "cols", scatter_dimension=2, tiled=True)

time: 1070 us -> 1380 us (1.29)
  blocking collectives: 120 us -> 408 us
  local copies, waits for them, and re-layouts: 25.8 us -> 39.9 us
    all_to_all x0 -> x2, blocking collectives: none -> 288 us  [body(): lax.all_to_all(jnp.stack([current] * lax.axis_size(('rows', 'cols'))), ('...]
    all_gather x4 -> x0, waiting for transfers between devices: 284 us -> none  [body(): gathered = lax.all_gather(current, ('rows', 'cols'), axis=2, tiled=True)]
    all_to_all x0 -> x2, waiting for transfers between devices: none -> 276 us  [body(): lax.all_to_all(jnp.stack([current] * lax.axis_size(('rows', 'cols'))), ('...]
  transfers between devices with their start and end apart: 9 -> 7, of which waited for: 9 -> 7; matrix products, arithmetic and copies ran while one was open for 1% -> 1% of each run, Pallas kernels for 0% -> 0%
where the time goes in v1:
time: 1380 us
  waiting for transfers between devices  490 us (36%)
  blocking collectives  408 us (30%)
  matrix products  322 us (23%)
  other arithmetic  87 us (6%)
  local copies, waits for them, and re-layouts  39.9 us (3%)
  between operations  15.2 us (1%)
    all_to_all x2, blocking collectives, body(): lax.all_to_all(jnp.stack([current] * lax.axis_size(('rows', 'cols'))), ('...  288 us
    all_to_all x2, waiting for transfers between devices, body(): lax.all_to_all(jnp.stack([current] * lax.axis_size(('rows', 'cols'))), ('...  276 us
    dot_general x4, matrix products, tile_product(): lax.dot_general(stacked, coupling[0], contract, precision=HIGH, preferred...  147 us
    dot_general x4, matrix products, tile_product(): lax.dot_general(stacked, coupling[1], contract, precision=HIGH, preferred...  144 us
    psum x1, waiting for transfers between devices, body(): lax.psum((pair_products(images, images), pair_products(current, images)),...  127 us
    psum x3, blocking collectives, body(): lax.psum((pair_products(images, images), pair_products(current, images)),...  120 us
    reduce_scatter x4, waiting for transfers between devices, body(): lax.psum_scatter(partial_value, 'cols', scatter_dimension=2, tiled=True)  87.7 us
    another operation x12, other arithmetic, orthonormal(): factor = jnp.linalg.cholesky(embedded)  37.8 us
  transfers between devices with their start and end apart: 7, of which 7 were waited for; matrix products, arithmetic and copies ran while one was open for 1% of the time, Pallas kernels for 0%

profile of v1, /device:TPU:0, one launch (start us, length us, event | category | flops | bytes accessed | tf_op | source)
XLA Modules:
  0.0 1375.5 jit_solution(14183722023837481648)
XLA Ops:
  8.3 3.5 stack.130
  11.8 7.4 all-to-all-start
  19.3 139.9 %all-to-all-done = f32[32,2,48,512]{3,2,1,0:T(8,128)} async-done(((f32[32,2,48,512]{3,2,1,0:T(8,128)}), f32[32,2,48,512]{3,2,1,0:T(8,128)}, u32[]{:S(2)}, u32[]{:S(2)}) %all-to-all-start) | async-done | bytes 6291488 | tf_op jit(solution)/shard_map/all_to_all | solution.py:61
  159.2 3.5 copy.58
  162.8 36.0 %fusion.6 = f32[96,2048]{1,0:T(8,128)S(1)} fusion(f32[96,4096]{1,0:T(8,128)S(1)} %bitcast.294, f32[2,2048,4096]{2,1,0:T(8,128)} %param.5), kind=kOutput, calls=%fused_computation.6 | convolution fusion | flops 9663676416 | bytes 35913728 | tf_op jit(solution)/shard_map/dot_general | solution.py:42
  198.8 36.7 %fusion.14 = f32[96,2048]{1,0:T(8,128)} fusion(f32[96,4096]{1,0:T(8,128)S(1)} %bitcast.295, f32[2,2048,4096]{2,1,0:T(8,128)} %param.5), kind=kOutput, calls=%fused_computation.14 | convolution fusion | flops 9663676416 | bytes 35913728 | tf_op jit(solution)/shard_map/dot_general | solution.py:39
  235.5 1.2 fusion.47
  237.7 24.4 %reduce-scatter.5.cloned.1.call-done = f32[2,48,512]{2,1,0:T(8,128)} async-done(((f32[2,48,2048]{2,1,0:T(8,128)}), f32[2,48,512]{2,1,0:T(8,128)}) %reduce-scatter.5.cloned.1.call-update) | async-done | bytes 196624 | tf_op jit(solution)/shard_map/reduce_scatter | solution.py:68
  262.1 1.2 fusion.80
  263.3 1.2 fusion.81
  264.5 1.2 fusion.38
  265.7 1.2 fusion.39
  266.9 40.0 %psum.56 = f32[2,48,48]{2,1,0:T(8,128)S(1)} all-reduce(f32[2,48,48]{2,1,0:T(8,128)S(1)} %pad_maximum_fusion.9), channel_id=1, replica_groups=mesh['rows'=8,'cols'=4] {'rows','cols'}, use_global_device_ids=true, to_apply=%region_1.0 | all-reduce | flops 4608 | bytes 36864 | tf_op jit(solution)/shard_map/psum | solution.py:69
  310.2 8.8 cholesky.74
  320.3 7.4 custom-call.8
  329.0 144.2 %all_to_all.20 = f32[32,2,48,512]{3,2,1,0:T(8,128)S(1)} all-to-all(f32[32,2,48,512]{3,2,1,0:T(8,128)S(1)} %stack.142), channel_id=1, replica_groups=mesh['rows'=8,'cols'=4] {'rows','cols'}, dimensions={0} | all-to-all | bytes 12582912 | tf_op jit(solution)/shard_map/all_to_all | solution.py:61
  474.3 36.0 %fusion.4 = f32[96,2048]{1,0:T(8,128)S(1)} fusion(f32[96,4096]{1,0:T(8,128)S(1)} %bitcast.296, f32[2,2048,4096]{2,1,0:T(8,128)} %param.5), kind=kOutput, calls=%fused_computation.4 | convolution fusion | flops 9663676416 | bytes 35913728 | tf_op jit(solution)/shard_map/dot_general | solution.py:42
  510.3 36.7 %fusion.12 = f32[96,2048]{1,0:T(8,128)} fusion(f32[96,4096]{1,0:T(8,128)S(1)} %bitcast.297, f32[2,2048,4096]{2,1,0:T(8,128)} %param.5), kind=kOutput, calls=%fused_computation.12 | convolution fusion | flops 9663676416 | bytes 35913728 | tf_op jit(solution)/shard_map/dot_general | solution.py:39
  547.0 1.2 fusion.45
  549.2 22.4 %reduce-scatter.7.cloned.1.call-done = f32[2,48,512]{2,1,0:T(8,128)} async-done(((f32[2,48,2048]{2,1,0:T(8,128)}), f32[2,48,512]{2,1,0:T(8,128)}) %reduce-scatter.7.cloned.1.call-update) | async-done | bytes 196624 | tf_op jit(solution)/shard_map/reduce_scatter | solution.py:68
  571.6 1.2 fusion.82
  572.8 1.2 fusion.83
  574.0 1.2 fusion.36
  575.2 1.2 fusion.37
  576.4 39.9 %psum.57 = f32[2,48,48]{2,1,0:T(8,128)S(1)} all-reduce(f32[2,48,48]{2,1,0:T(8,128)S(1)} %pad_maximum_fusion.10), channel_id=1, replica_groups=mesh['rows'=8,'cols'=4] {'rows','cols'}, use_global_device_ids=true, to_apply=%region_5.8 | all-reduce | flops 4608 | bytes 36864 | tf_op jit(solution)/shard_map/psum | solution.py:69
  618.3 1.7 copy.38
  619.9 1.5 reshape.144
  623.1 8.8 cholesky.85
  633.2 7.4 custom-call.9
  641.9 143.9 %all_to_all.21 = f32[32,2,48,512]{3,2,1,0:T(8,128)S(1)} all-to-all(f32[32,2,48,512]{3,2,1,0:T(8,128)S(1)} %stack.154), channel_id=1, replica_groups=mesh['rows'=8,'cols'=4] {'rows','cols'}, dimensions={0} | all-to-all | bytes 12582912 | tf_op jit(solution)/shard_map/all_to_all | solution.py:61
  787.0 36.0 %fusion.2 = f32[96,2048]{1,0:T(8,128)S(1)} fusion(f32[96,4096]{1,0:T(8,128)S(1)} %bitcast.298, f32[2,2048,4096]{2,1,0:T(8,128)} %param.5), kind=kOutput, calls=%fused_computation.2 | convolution fusion | flops 9663676416 | bytes 35913728 | tf_op jit(solution)/shard_map/dot_general | solution.py:42
  823.0 36.9 %fusion.10 = f32[96,2048]{1,0:T(8,128)} fusion(f32[96,4096]{1,0:T(8,128)S(1)} %bitcast.299, f32[2,2048,4096]{2,1,0:T(8,128)} %param.5), kind=kOutput, calls=%fused_computation.10 | convolution fusion | flops 9663676416 | bytes 35913728 | tf_op jit(solution)/shard_map/dot_general | solution.py:39
  860.0 1.2 fusion.43
  862.1 22.5 %reduce-scatter.9.cloned.1.call-done = f32[2,48,512]{2,1,0:T(8,128)} async-done(((f32[2,48,2048]{2,1,0:T(8,128)}), f32[2,48,512]{2,1,0:T(8,128)}) %reduce-scatter.9.cloned.1.call-update) | async-done | bytes 196624 | tf_op jit(solution)/shard_map/reduce_scatter | solution.py:68
  884.6 1.2 fusion.84
  885.8 1.2 fusion.85
  887.0 1.2 fusion.34
  888.2 1.2 fusion.35
  889.4 39.9 %psum.58 = f32[2,48,48]{2,1,0:T(8,128)S(1)} all-reduce(f32[2,48,48]{2,1,0:T(8,128)S(1)} %pad_maximum_fusion.11), channel_id=1, replica_groups=mesh['rows'=8,'cols'=4] {'rows','cols'}, use_global_device_ids=true, to_apply=%region_7.10 | all-reduce | flops 4608 | bytes 36864 | tf_op jit(solution)/shard_map/psum | solution.py:69
  931.2 1.7 copy.43
  932.9 1.5 reshape.150
  936.0 8.8 cholesky.96
  946.2 7.4 custom-call.10
  954.7 3.5 stack.166
  958.2 5.4 all-to-all-start.3
  967.7 135.9 %all-to-all-done.3 = f32[32,2,48,512]{3,2,1,0:T(8,128)} async-done(((f32[32,2,48,512]{3,2,1,0:T(8,128)}), f32[32,2,48,512]{3,2,1,0:T(8,128)}, u32[]{:S(2)}, u32[]{:S(2)}) %all-to-all-start.3) | async-done | bytes 6291488 | tf_op jit(solution)/shard_map/all_to_all | solution.py:61
  1103.6 3.5 copy.61
  1107.2 36.2 %fusion = f32[96,2048]{1,0:T(8,128)S(1)} fusion(f32[96,4096]{1,0:T(8,128)S(1)} %bitcast.292, f32[2,2048,4096]{2,1,0:T(8,128)} %param.5), kind=kOutput, calls=%fused_computation | convolution fusion | flops 9663676416 | bytes 35913728 | tf_op jit(solution)/shard_map/dot_general | solution.py:42
  1143.4 36.7 %fusion.8 = f32[96,2048]{1,0:T(8,128)} fusion(f32[96,4096]{1,0:T(8,128)S(1)} %bitcast.293, f32[2,2048,4096]{2,1,0:T(8,128)} %param.5), kind=kOutput, calls=%fused_computation.8 | convolution fusion | flops 9663676416 | bytes 35913728 | tf_op jit(solution)/shard_map/dot_general | solution.py:39
  1180.1 1.2 fusion.41
  1182.7 1.1 fusion.29
  1183.8 1.1 fusion.28
  1185.6 1.2 fusion.119
  1188.5 18.3 %reduce-scatter.11.cloned.1.call-done = f32[2,48,512]{2,1,0:T(8,128)} async-done(((f32[2,48,2048]{2,1,0:T(8,128)}), f32[2,48,512]{2,1,0:T(8,128)}) %reduce-scatter.11.cloned.1.call-update) | async-done | bytes 196624 | tf_op jit(solution)/shard_map/reduce_scatter | solution.py:68
  1207.9 1.1 fusion.52
  1209.1 1.1 fusion.25
  1210.2 1.1 fusion.24
  1211.9 1.2 fusion.86
  1213.1 1.2 fusion.87
  1214.3 1.2 fusion.32
  1215.5 1.2 fusion.33
  1218.6 126.8 %all-reduce.3.cloned.1.call-done = (f32[2,48,48]{2,1,0:T(8,128)}, f32[2,48,48]{2,1,0:T(8,128)}, f32[2,48,48]{2,1,0:T(8,128)}, f32[2,48,48]{2,1,0:T(8,128)}, f32[2,48,48]{2,1,0:T(8,128)}) async-done(((f32[2,48,48]{2,1,0:T(8,128)}, f32[2,48,48]{2,1,0:T(8,128)}, f32[2,48,48]{2,1,0:T(8,128)}, f32[2,48,48]{2,1,0:T(8,128)}, f32[2,48,48]{2,1,0:T(8,128)}), (f32[2,48,48]{2,1,0:T(8,128)}, f32[2,48,48]{2,1,0:T(8,128)}, ...) | async-done | bytes 92176 | tf_op jit(solution)/shard_map/psum | solution.py:69
  1348.3 8.8 cholesky.107
  1358.4 7.4 custom-call.11
  (129 shorter events, 42.9 us)
Async XLA Ops:
  7.2 1.1 copy-start
  11.8 147.4 %all-to-all-start = ((f32[32,2,48,512]{3,2,1,0:T(8,128)}), f32[32,2,48,512]{3,2,1,0:T(8,128)}, u32[]{:S(2)}, u32[]{:S(2)}) async-start(f32[32,2,48,512]{3,2,1,0:T(8,128)} %stack.130), calls=%async_computation | async-start | bytes 12582912 | tf_op jit(solution)/shard_map/all_to_all | solution.py:61
  19.2 242.9 %reduce-scatter.5.cloned.1.call-start = ((), (), s32[]{:S(2)}) async-start(), calls=%async_computation.8 | async-start | bytes 983040 | tf_op jit(solution)/shard_map/reduce_scatter | solution.py:68
  237.7 334.0 %reduce-scatter.7.cloned.1.call-start = ((), (), s32[]{:S(2)}) async-start(), calls=%async_computation.9 | async-start | bytes 983040 | tf_op jit(solution)/shard_map/reduce_scatter | solution.py:68
  549.1 335.5 %reduce-scatter.9.cloned.1.call-start = ((), (), s32[]{:S(2)}) async-start(), calls=%async_computation.10 | async-start | bytes 983040 | tf_op jit(solution)/shard_map/reduce_scatter | solution.py:68
  641.1 144.8 %copy-start.4 = (f32[48,2,512]{2,1,0:T(2,128)}, f32[48,2,512]{2,1,0:T(2,128)S(1)}, u32[]{:S(2)}) copy-start(f32[48,2,512]{2,1,0:T(2,128)S(1)} %reshape.146) | copy-start | bytes 589828
  954.0 0.7 copy-start.5
  958.2 5.5 copy-start.1
  958.2 7.9 copy-start.2
  958.2 145.4 %all-to-all-start.3 = ((f32[32,2,48,512]{3,2,1,0:T(8,128)}), f32[32,2,48,512]{3,2,1,0:T(8,128)}, u32[]{:S(2)}, u32[]{:S(2)}) async-start(f32[32,2,48,512]{3,2,1,0:T(8,128)} %stack.166), calls=%async_computation.6 | async-start | bytes 12582912 | tf_op jit(solution)/shard_map/all_to_all | solution.py:61
  963.6 243.2 %reduce-scatter.11.cloned.1.call-start = ((), (), s32[]{:S(2)}) async-start(), calls=%async_computation.11 | async-start | bytes 983040 | tf_op jit(solution)/shard_map/reduce_scatter | solution.py:68
  1143.4 43.4 %copy-start.3 = (f32[2,48,512]{2,1,0:T(8,128)S(1)}, f32[2,48,512]{2,1,0:T(8,128)}, u32[]{:S(2)}) copy-start(f32[2,48,512]{2,1,0:T(8,128)} %reduce-scatter.9.cloned.1.call-done) | copy-start | bytes 589828
  1180.1 8.2 copy-start.6
  1182.3 163.1 %all-reduce.3.cloned.1.call-start = ((), (), s32[]{:S(2)}) async-start(), calls=%async_computation.12 | async-start | bytes 491520 | tf_op jit(solution)/shard_map/psum | solution.py:69
  1345.4 22.3 %copy-start.7 = (f32[2,48,48]{2,1,0:T(8,128)S(1)}, f32[2,48,48]{2,1,0:T(8,128)}, u32[]{:S(2)}) copy-start(f32[2,48,48]{2,1,0:T(8,128)} %get-tuple-element.7) | copy-start | bytes 55300
  1345.4 22.4 %copy-start.8 = (f32[2,48,48]{2,1,0:T(8,128)S(1)}, f32[2,48,48]{2,1,0:T(8,128)}, u32[]{:S(2)}) copy-start(f32[2,48,48]{2,1,0:T(8,128)} %get-tuple-element.8) | copy-start | bytes 55300
Sparse Core Ops, SparseCore 0:
  237.8 24.3 reduce-scatter.4
  549.3 22.3 reduce-scatter.6
  862.2 22.3 reduce-scatter.8
  1182.5 24.3 reduce-scatter.10
  1217.5 127.9 all-reduce.2
